TPU v7x, 32 devices: a whole 2x2x4 slice. The times are simulated.
32 devices in a mesh: groups: 2 (over y), blk: 4 (over z), heads: 2 (over x), sub: 2 (over core).
Axes of the slice: x: 2, y: 2, z: 4, core: 2. Of those that a mesh axis runs over, the one named last changes fastest.
Arguments:
- queries: bfloat16 [8, 64, 8, 8, 128], P(('groups', 'sub'), 'blk', 'heads'), parts along dimension 0, may hold values from -30 to 30
- key_pool: bfloat16 [256, 128, 8, 128], P(('groups', 'blk', 'sub'), None, 'heads'), parts along dimension 0, may hold values from -15 to 15
- value_pool: bfloat16 [256, 128, 8, 128], P(('groups', 'blk', 'sub'), None, 'heads'), parts along dimension 0, may hold values from -6 to 6
- page_table: int32 [8, 32], P(('groups', 'sub'), 'blk'), parts along dimension 0, may hold values from 0 to 15, as said below
- cache_lengths: int32 [8], P(('groups', 'sub')), parts along dimension 0, may hold values from 1024 to 4096
- tree_sizes: int32 [8], P(('groups', 'sub')), parts along dimension 0, may hold values from 16 to 64
- ancestor_bits: int32 [8, 64, 2], P(('groups', 'sub'), 'blk'), parts along dimension 0, may hold values from -2147483648 to 2147483647, as said below
- tree_keys: bfloat16 [8, 64, 8, 128], P(('groups', 'sub'), 'blk', 'heads'), parts along dimension 0, may hold values from -17 to 17
- tree_values: bfloat16 [8, 64, 8, 128], P(('groups', 'sub'), 'blk', 'heads'), parts along dimension 0, may hold values from -6 to 6
Outputs:
- attended: bfloat16 [8, 64, 8, 8, 128], P(('groups', 'sub'), 'blk', 'heads'), parts along dimension 0
There are 2 independent parts, one for each index of `groups`. A program takes and returns all parts, laid end to end along the dimension named above; each array names one. Nothing has to cross between parts.
Inputs may be any that keep to these rules, and one draw needn't show every extreme that they name: `page_table`: within the rows of requests s * 2 to (s + 1) * 2 - 1 and the columns b * 8 to (b + 1) * 8 - 1, the entries are a permutation of 0 to 15. `ancestor_bits`: bit k % 32 of word k // 32 of row n is 1 exactly when node k is n or an ancestor of n; every node n > 0 has one parent with a lower number; bits for k >= 64 are 0; bit 31 is the sign bit of the word.
All inputs are finite; a program needn't handle non-finite values.
Results may differ from a plain program's by a relative error of at most 0.0055.
Values may be sent and summed in bfloat16 or wider, within the bound.
A program may use at most 64 MiB of HBM per device.

v0:
```python
import math

import jax
import jax.numpy as jnp
from jax import lax
from jax.sharding import PartitionSpec as P

BLOCKED = -1e30


def absorb(carry, query_rows, keys, values, live_mask, score_scale):
    row_top, totals, weighted = carry
    scores = (
        jnp.einsum("rnhgd,rchd->rhngc", query_rows, keys, preferred_element_type=jnp.float32)
        * score_scale
    )
    scores = jnp.where(live_mask, scores, BLOCKED)
    new_top = jnp.maximum(row_top, jnp.max(scores, axis=-1))
    factor = jnp.exp(row_top - new_top)
    weights = jnp.where(live_mask, jnp.exp(scores - new_top[..., None]), 0.0)
    totals = totals * factor + jnp.sum(weights, axis=-1)
    weighted = weighted * factor[..., None] + jnp.einsum(
        "rhngc,rchd->rhngd",
        weights.astype(jnp.bfloat16),
        values,
        preferred_element_type=jnp.float32,
    )
    return (new_top, totals, weighted)


def attend_cache(carry, query_rows, keys, values, first_position, lengths, block_len, score_scale):
    block_count = keys.shape[1] // block_len

    def attend_one_block(block_at, inner):
        key_block = lax.dynamic_slice_in_dim(keys, block_at * block_len, block_len, 1)
        value_block = lax.dynamic_slice_in_dim(values, block_at * block_len, block_len, 1)
        positions = first_position + block_at * block_len + jnp.arange(block_len, dtype=jnp.int32)
        live_mask = (positions[None, :] < lengths[:, None])[:, None, None, None, :]
        return absorb(inner, query_rows, key_block, value_block, live_mask, score_scale)

    return lax.fori_loop(0, block_count, attend_one_block, carry)


def cache_maxima(initial, query_rows, keys, first_position, lengths, block_len, score_scale):
    block_count = keys.shape[1] // block_len

    def cache_one_block(block_at, running):
        key_block = lax.dynamic_slice_in_dim(keys, block_at * block_len, block_len, 1)
        positions = first_position + block_at * block_len + jnp.arange(block_len, dtype=jnp.int32)
        live_mask = (positions[None, :] < lengths[:, None])[:, None, None, None, :]
        scores = (
            jnp.einsum(
                "rnhgd,rchd->rhngc", query_rows, key_block, preferred_element_type=jnp.float32
            )
            * score_scale
        )
        scores = jnp.where(live_mask, scores, BLOCKED)
        return jnp.maximum(running, jnp.max(scores, axis=-1))

    return lax.fori_loop(0, block_count, cache_one_block, initial)


def shards(
    queries,
    key_pool,
    value_pool,
    page_table,
    cache_lengths,
    tree_sizes,
    ancestor_bits,
    tree_keys,
    tree_values,
):
    requests, nodes_dev, heads_dev, group_size, head_dim = queries.shape
    score_scale = 1.0 / math.sqrt(head_dim)
    page_len = key_pool.shape[1]
    cache_dev = page_table.shape[1] * page_len
    slot_rows = page_table.reshape(-1)
    cache_keys = jnp.take(key_pool, slot_rows, axis=0).reshape(
        requests, cache_dev, heads_dev, head_dim
    )
    cache_values = jnp.take(value_pool, slot_rows, axis=0).reshape(
        requests, cache_dev, heads_dev, head_dim
    )
    blk_at = lax.axis_index("blk")
    first_node = blk_at * nodes_dev
    tree_all_keys, tree_all_values = (
        lax.all_gather(tree_keys, "blk", axis=1, tiled=True),
        lax.all_gather(tree_values, "blk", axis=1, tiled=True),
    )
    total_nodes = tree_all_keys.shape[1]
    node_ids = first_node + jnp.arange(nodes_dev, dtype=jnp.int32)
    node_valid = node_ids[None, :] < tree_sizes[:, None]
    shifts = jnp.arange(32, dtype=jnp.int32)
    bit_table = jnp.bitwise_and(jnp.right_shift(ancestor_bits[..., None], shifts), 1)
    bit_table = bit_table.reshape(requests, nodes_dev, -1)
    key_nodes = jnp.arange(total_nodes, dtype=jnp.int32)
    allowed = (bit_table > 0) & (key_nodes[None, None, :] < tree_sizes[:, None, None])
    tree_mask = allowed[:, None, :, None, :]
    everyone = lax.all_gather(queries, "blk", axis=1, tiled=True)
    empty_top = jnp.full((requests, heads_dev, total_nodes, group_size), BLOCKED, jnp.float32)
    local_top = cache_maxima(
        empty_top, everyone, cache_keys, blk_at * cache_dev, cache_lengths, page_len, score_scale
    )
    tree_scores = (
        jnp.einsum("rnhgd,rchd->rhngc", queries, tree_all_keys, preferred_element_type=jnp.float32)
        * score_scale
    )
    own_tree_top = jnp.max(jnp.where(tree_mask, tree_scores, BLOCKED), axis=-1)
    tree_top = lax.dynamic_update_slice_in_dim(empty_top, own_tree_top, first_node, 2)
    row_top = lax.pmax(jnp.maximum(local_top, tree_top), "blk")
    start_state = (
        row_top,
        jnp.zeros((requests, heads_dev, total_nodes, group_size), jnp.float32),
        jnp.zeros((requests, heads_dev, total_nodes, group_size, head_dim), jnp.float32),
    )
    same_top, local_total, local_sum = attend_cache(
        start_state,
        everyone,
        cache_keys,
        cache_values,
        blk_at * cache_dev,
        cache_lengths,
        page_len,
        score_scale,
    )
    totals, weighted = (
        lax.psum_scatter(local_total, "blk", scatter_dimension=2, tiled=True),
        lax.psum_scatter(local_sum, "blk", scatter_dimension=2, tiled=True),
    )
    own_top = lax.dynamic_slice_in_dim(same_top, first_node, nodes_dev, 2)
    carry = (own_top, totals, weighted)
    carry = absorb(carry, queries, tree_all_keys, tree_all_values, tree_mask, score_scale)
    row_top, totals, weighted = carry
    attended = weighted / totals[..., None]
    attended = jnp.where(node_valid[:, None, :, None, None], attended, 0.0)
    return attended.astype(jnp.bfloat16).transpose(0, 2, 1, 3, 4)


def solution(mesh):
    placed = (
        P(("groups", "sub"), "blk", "heads", None, None),
        P(("groups", "blk", "sub"), None, "heads", None),
        P(("groups", "blk", "sub"), None, "heads", None),
        P(("groups", "sub"), "blk"),
        P(("groups", "sub")),
        P(("groups", "sub")),
        P(("groups", "sub"), "blk", None),
        P(("groups", "sub"), "blk", "heads", None),
        P(("groups", "sub"), "blk", "heads", None),
    )
    return jax.shard_map(
        shards,
        mesh=mesh,
        in_specs=placed,
        out_specs=P(("groups", "sub"), "blk", "heads", None, None),
        check_vma=False,
    )
```

profile of v0, /device:TPU:0, one launch (start us, length us, event | category | flops | bytes accessed | tf_op | source)
XLA Modules:
  0.0 216.5 jit_solution(17230364504249146826)
XLA Ops:
  6.5 1.9 copy.54
  8.5 0.8 reshape.140
  9.3 3.5 %gather_fusion.1 = bf16[16,128,4,128]{3,2,1,0:T(4,128)(2,1)} fusion(bf16[16,128,4,128]{3,2,1,0:T(4,128)(2,1)S(1)} %copy-done, s32[1024]{0:T(1024)S(1)} %pad_clamp_fusion), kind=kCustom, calls=%fused_computation.1.clone | custom fusion | bytes 4194368 | tf_op jit(solution)/shard_map/jit(_take)/gather | solution.py:82
  12.9 5.2 %gather_fusion = bf16[16,128,4,128]{3,2,1,0:T(4,128)(2,1)} fusion(bf16[16,128,4,128]{3,2,1,0:T(4,128)(2,1)} %param.16, s32[1024]{0:T(1024)S(1)} %pad_clamp_fusion), kind=kCustom, calls=%fused_computation.clone | custom fusion | bytes 4194368 | tf_op jit(solution)/shard_map/jit(_take)/gather | solution.py:79
  18.0 5.5 %broadcast_select_fusion = (bf16[16,128,4,128]{3,2,1,0:T(4,128)(2,1)}, bf16[16,128,4,128]{3,2,1,0:T(4,128)(2,1)S(1)}) fusion(bf16[16,128,4,128]{3,2,1,0:T(4,128)(2,1)} %gather_fusion.1, pred[16]{0:T(512)(128)(4,1)S(1)} %compare_and_fusion, bf16[16,128,4,128]{3,2,1,0:T(4,128)(2,1)} %gather_fusion), kind=kLoop, calls=%fused_computation.31 | loop fusion | flops 2097152 | bytes 8388624 | tf_op jit(solution)/shard_map/jit(_take)/select_n | solution.py:82
  23.6 0.5 copy.53
  24.2 1.5 copy.55
  26.0 15.9 %all_gather.10 = bf16[2,64,4,128]{3,1,2,0:T(8,128)(2,1)S(1)} all-gather(bf16[2,16,4,128]{3,1,2,0:T(8,128)(2,1)S(1)} %copy.57), channel_id=1, replica_groups=mesh['groups'=2,'blk'=4,'heads'=2,'sub'=2] {'blk'}, dimensions={1}, use_global_device_ids=true | all-gather | bytes 163840 | tf_op jit(solution)/shard_map/all_gather | solution.py:88
  42.0 1.0 fusion.31
  43.3 0.3 all-gather.2.cloned.1.call-done
  43.6 17.8 %while.32 = (s32[]{:T(128)}, f32[2,4,64,8]{2,3,1,0:T(8,128)S(1)}, s32[]{:T(128)}, s32[2]{0:T(128)S(1)}, bf16[2,1024,4,128]{3,1,2,0:T(8,128)(2,1)}, /*index=5*/bf...) while((s32[]{:T(128)}, f32[2,4,64,8]{2,3,1,0:T(8,128)S(1)}, ...), condition=%wide.region_2.4_spmd.clone, body=%wide.region_0.3_spmd.clone.sunk | while | flops 135795072 | bytes 1377985 | solution.py:60
  43.7 2.1 select_reduce_fusion.2
  46.0 2.1 select_reduce_fusion.2
  48.2 2.1 select_reduce_fusion.2
  50.4 2.1 select_reduce_fusion.2
  52.6 2.1 select_reduce_fusion.2
  54.9 2.1 select_reduce_fusion.2
  57.1 2.1 select_reduce_fusion.2
  59.3 2.1 select_reduce_fusion.2
  61.5 19.9 %pmax.7 = f32[2,4,64,8]{2,3,1,0:T(8,128)S(1)} all-reduce(f32[2,4,64,8]{2,3,1,0:T(8,128)S(1)} %max.22), channel_id=1, replica_groups=mesh['groups'=2,'blk'=4,'heads'=2,'sub'=2] {'blk'}, use_global_device_ids=true, to_apply=%region_4.6 | all-reduce | flops 4096 | bytes 32768 | tf_op jit(solution)/shard_map/pmax | solution.py:111
  81.4 63.3 %while.33 = (s32[]{:T(128)}, f32[2,4,64,8]{2,3,1,0:T(8,128)S(1)}, f32[2,4,64,8]{2,3,1,0:T(8,128)S(1)}, f32[2,4,64,8,128]{4,3,2,1,0:T(8,128)}, s32[]{:T(128)}, /*...) while((s32[]{:T(128)}, f32[2,4,64,8]{2,3,1,0:T(8,128)S(1)}, ...), condition=%wide.region_8.10_spmd.clone, body=%wide.region_5.9_spmd.clone.sunk | while | flops 274739584 | bytes 12863454 | solution.py:41
  81.5 2.1 bitcast_reduce_fusion.2
  83.7 1.4 fusion.45
  85.2 1.1 constant_dynamic-slice_fusion.2
  86.3 2.0 fusion.47
  88.4 2.1 bitcast_reduce_fusion.2
  90.5 1.4 fusion.45
  92.1 1.1 constant_dynamic-slice_fusion.2
  93.1 3.2 %fusion.47 = f32[2,4,64,8,128]{4,3,2,1,0:T(8,128)} fusion(f32[2,4,64,8,128]{4,3,2,1,0:T(8,128)} %get-tuple-element.563, bf16[2,4,64,8,128]{4,2,3,1,0:T(8,128)(2,1)S(1)} %get-tuple-element.515, f32[2,4,64,8]{3,2,1,0:T(8,128)S(1)} %copy.103, pred[]{:T(512)S(6)} %compare.7, bf16[2,128,4,128]{3,2,1,0:T(4,128)(2,1)S(1)} %constant_dynamic-slice_fusion.2), kind=kOutput, calls=%fused_computation.14.clone.1 | convolution fusion | flops 135790592 | bytes 5521409 | tf_op jit(solution)/shard_map/while/body/eval_jaxpr/rhngc,rchd->rhngd/dot_general | solution.py:22
  96.5 2.1 bitcast_reduce_fusion.2
  98.6 1.4 fusion.45
  100.1 1.1 constant_dynamic-slice_fusion.2
  101.2 3.2 %fusion.47 = f32[2,4,64,8,128]{4,3,2,1,0:T(8,128)} fusion(f32[2,4,64,8,128]{4,3,2,1,0:T(8,128)} %get-tuple-element.563, bf16[2,4,64,8,128]{4,2,3,1,0:T(8,128)(2,1)S(1)} %get-tuple-element.515, f32[2,4,64,8]{3,2,1,0:T(8,128)S(1)} %copy.103, pred[]{:T(512)S(6)} %compare.7, bf16[2,128,4,128]{3,2,1,0:T(4,128)(2,1)S(1)} %constant_dynamic-slice_fusion.2), kind=kOutput, calls=%fused_computation.14.clone.1 | convolution fusion | flops 135790592 | bytes 5521409 | tf_op jit(solution)/shard_map/while/body/eval_jaxpr/rhngc,rchd->rhngd/dot_general | solution.py:22
  104.5 2.1 bitcast_reduce_fusion.2
  106.7 1.4 fusion.45
  108.2 1.1 constant_dynamic-slice_fusion.2
  109.3 3.2 %fusion.47 = f32[2,4,64,8,128]{4,3,2,1,0:T(8,128)} fusion(f32[2,4,64,8,128]{4,3,2,1,0:T(8,128)} %get-tuple-element.563, bf16[2,4,64,8,128]{4,2,3,1,0:T(8,128)(2,1)S(1)} %get-tuple-element.515, f32[2,4,64,8]{3,2,1,0:T(8,128)S(1)} %copy.103, pred[]{:T(512)S(6)} %compare.7, bf16[2,128,4,128]{3,2,1,0:T(4,128)(2,1)S(1)} %constant_dynamic-slice_fusion.2), kind=kOutput, calls=%fused_computation.14.clone.1 | convolution fusion | flops 135790592 | bytes 5521409 | tf_op jit(solution)/shard_map/while/body/eval_jaxpr/rhngc,rchd->rhngd/dot_general | solution.py:22
  112.6 2.1 bitcast_reduce_fusion.2
  114.7 1.4 fusion.45
  116.3 1.1 constant_dynamic-slice_fusion.2
  117.3 3.2 %fusion.47 = f32[2,4,64,8,128]{4,3,2,1,0:T(8,128)} fusion(f32[2,4,64,8,128]{4,3,2,1,0:T(8,128)} %get-tuple-element.563, bf16[2,4,64,8,128]{4,2,3,1,0:T(8,128)(2,1)S(1)} %get-tuple-element.515, f32[2,4,64,8]{3,2,1,0:T(8,128)S(1)} %copy.103, pred[]{:T(512)S(6)} %compare.7, bf16[2,128,4,128]{3,2,1,0:T(4,128)(2,1)S(1)} %constant_dynamic-slice_fusion.2), kind=kOutput, calls=%fused_computation.14.clone.1 | convolution fusion | flops 135790592 | bytes 5521409 | tf_op jit(solution)/shard_map/while/body/eval_jaxpr/rhngc,rchd->rhngd/dot_general | solution.py:22
  120.6 2.1 bitcast_reduce_fusion.2
  122.8 1.4 fusion.45
  124.3 1.1 constant_dynamic-slice_fusion.2
  125.4 3.2 %fusion.47 = f32[2,4,64,8,128]{4,3,2,1,0:T(8,128)} fusion(f32[2,4,64,8,128]{4,3,2,1,0:T(8,128)} %get-tuple-element.563, bf16[2,4,64,8,128]{4,2,3,1,0:T(8,128)(2,1)S(1)} %get-tuple-element.515, f32[2,4,64,8]{3,2,1,0:T(8,128)S(1)} %copy.103, pred[]{:T(512)S(6)} %compare.7, bf16[2,128,4,128]{3,2,1,0:T(4,128)(2,1)S(1)} %constant_dynamic-slice_fusion.2), kind=kOutput, calls=%fused_computation.14.clone.1 | convolution fusion | flops 135790592 | bytes 5521409 | tf_op jit(solution)/shard_map/while/body/eval_jaxpr/rhngc,rchd->rhngd/dot_general | solution.py:22
  128.7 2.1 bitcast_reduce_fusion.2
  130.8 1.4 fusion.45
  132.4 1.1 constant_dynamic-slice_fusion.2
  133.5 3.2 %fusion.47 = f32[2,4,64,8,128]{4,3,2,1,0:T(8,128)} fusion(f32[2,4,64,8,128]{4,3,2,1,0:T(8,128)} %get-tuple-element.563, bf16[2,4,64,8,128]{4,2,3,1,0:T(8,128)(2,1)S(1)} %get-tuple-element.515, f32[2,4,64,8]{3,2,1,0:T(8,128)S(1)} %copy.103, pred[]{:T(512)S(6)} %compare.7, bf16[2,128,4,128]{3,2,1,0:T(4,128)(2,1)S(1)} %constant_dynamic-slice_fusion.2), kind=kOutput, calls=%fused_computation.14.clone.1 | convolution fusion | flops 135790592 | bytes 5521409 | tf_op jit(solution)/shard_map/while/body/eval_jaxpr/rhngc,rchd->rhngd/dot_general | solution.py:22
  136.8 2.1 bitcast_reduce_fusion.2
  138.9 1.4 fusion.45
  140.5 1.1 constant_dynamic-slice_fusion.2
  141.5 3.2 %fusion.47 = f32[2,4,64,8,128]{4,3,2,1,0:T(8,128)} fusion(f32[2,4,64,8,128]{4,3,2,1,0:T(8,128)} %get-tuple-element.563, bf16[2,4,64,8,128]{4,2,3,1,0:T(8,128)(2,1)S(1)} %get-tuple-element.515, f32[2,4,64,8]{3,2,1,0:T(8,128)S(1)} %copy.103, pred[]{:T(512)S(6)} %compare.7, bf16[2,128,4,128]{3,2,1,0:T(4,128)(2,1)S(1)} %constant_dynamic-slice_fusion.2), kind=kOutput, calls=%fused_computation.14.clone.1 | convolution fusion | flops 135790592 | bytes 5521409 | tf_op jit(solution)/shard_map/while/body/eval_jaxpr/rhngc,rchd->rhngd/dot_general | solution.py:22
  144.9 0.8 reshape.172
  146.0 1.9 copy.74
  147.9 2.5 %copy.97 = f32[8,8,64,128]{3,1,2,0:T(8,128)} copy(f32[8,8,64,128]{3,2,1,0:T(8,128)S(1)} %bitcast.78) | data formatting | bytes 4194304
  150.4 0.7 copy-done.6
  151.2 13.4 %all_gather.11 = bf16[2,64,4,128]{3,1,2,0:T(8,128)(2,1)S(1)} all-gather(bf16[2,16,4,128]{3,1,2,0:T(8,128)(2,1)S(1)} %copy.64), channel_id=1, replica_groups=mesh['groups'=2,'blk'=4,'heads'=2,'sub'=2] {'blk'}, dimensions={1}, use_global_device_ids=true | all-gather | bytes 163840 | tf_op jit(solution)/shard_map/all_gather | solution.py:89
  164.8 0.4 fusion.19
  165.2 0.8 reshape.173
  166.1 41.5 %reduce-scatter.8.cloned.1.call-done = f32[16,8192]{1,0:T(8,128)} async-done(((f32[64,8192]{1,0:T(8,128)}), f32[16,8192]{1,0:T(8,128)}) %reduce-scatter.8.cloned.1.call-update) | async-done | bytes 524304
  207.6 1.1 copy.81
  208.7 0.5 fusion.18
  209.2 0.7 copy.66
  (123 shorter events, 4.1 us)
Async XLA Ops:
  6.5 2.8 %copy-start = (bf16[16,128,4,128]{3,2,1,0:T(4,128)(2,1)S(1)}, bf16[16,128,4,128]{3,2,1,0:T(4,128)(2,1)}, u32[]{:S(2)}) copy-start(bf16[16,128,4,128]{3,2,1,0:T(4,128)(2,1)} %param.17) | copy-start | bytes 6291460
  6.5 37.1 %all-gather.2.cloned.1.call-start = ((), (), s32[]{:S(2)}) async-start(), calls=%async_computation.2 | async-start | bytes 1310720 | tf_op jit(solution)/shard_map/all_gather | solution.py:100
  8.5 156.8 %reduce-scatter.10.cloned.1.call-start = ((), (), s32[]{:S(2)}) async-start(), calls=%async_computation.4 | async-start | bytes 40960
  24.1 1.5 copy-start.5
  24.1 1.5 copy-start.7
  24.1 17.8 %copy-start.9 = (s32[2]{0:T(128)S(1)}, s32[2]{0:T(128)}, u32[]{:S(2)}) copy-start(s32[2]{0:T(128)} %param.20) | copy-start | bytes 28
  24.1 17.8 %copy-start.2 = (bf16[2,16,4,8,128]{4,3,2,1,0:T(8,128)(2,1)S(1)}, bf16[2,16,4,8,128]{4,3,2,1,0:T(8,128)(2,1)}, u32[]{:S(2)}) copy-start(bf16[2,16,4,8,128]{4,3,2,1,0:T(8,128)(2,1)} %param.15) | copy-start | bytes 786436
  24.2 19.5 %copy-start.8 = (s32[2]{0:T(128)S(1)}, s32[2]{0:T(128)}, u32[]{:S(2)}) copy-start(s32[2]{0:T(128)} %param.19) | copy-start | bytes 28
  43.0 0.7 copy-start.3
  145.8 61.8 %reduce-scatter.8.cloned.1.call-start = ((), (), s32[]{:S(2)}) async-start(), calls=%async_computation.3 | async-start | bytes 2621440
  150.4 0.8 copy-start.6
  150.4 14.4 %copy-start.4 = (f32[2,4,16,8]{3,2,1,0:T(8,128)S(1)}, f32[2,4,16,8]{3,2,1,0:T(8,128)}, u32[]{:S(2)}) copy-start(f32[2,4,16,8]{3,2,1,0:T(8,128)} %copy-done.3) | copy-start | bytes 12292
  150.4 14.4 %copy-start.1 = (f32[2,4,16,8,64]{4,3,2,1,0:T(8,128)S(1)}, f32[2,4,16,8,64]{4,3,2,1,0:T(8,128)}, u32[]{:S(2)}) copy-start(f32[2,4,16,8,64]{4,3,2,1,0:T(8,128)} %get-tuple-element.412) | copy-start | bytes 786436
Sparse Core Ops, SparseCore 0:
  8.9 34.6 all-gather.1
  145.9 17.5 reduce-scatter.9
  165.8 41.7 reduce-scatter.7
where the time goes:
time: 218 us; the launch traced here: 217 us
  matrix products  59.9 us (27%)
  blocking collectives  49.2 us (23%)
  waiting for transfers between devices  41.9 us (19%)
  local copies, waits for them, and re-layouts  32.4 us (15%)
  other arithmetic  18.7 us (9%)
  between operations  13.4 us (6%)
    unnamed x5, waiting for transfers between devices  41.6 us
    dot_general x9, matrix products, absorb(): jnp.einsum('rhngc,rchd->rhngd', weights.astype(jnp.bfloat16), values, pre...  25.2 us
    pmax x1, blocking collectives, shards(): row_top = lax.pmax(jnp.maximum(local_top, tree_top), 'blk')  19.9 us
    dot_general x8, matrix products, absorb(): jnp.einsum('rnhgd,rchd->rhngc', query_rows, keys, preferred_element_type=...  16.9 us
    dot_general x8, matrix products, cache_one_block(): jnp.einsum('rnhgd,rchd->rhngc', query_rows, key_block, preferred_element_...  16.8 us
    all_gather x1, blocking collectives, shards(): lax.all_gather(tree_keys, 'blk', axis=1, tiled=True)  15.9 us
    all_gather x1, blocking collectives, shards(): lax.all_gather(tree_values, 'blk', axis=1, tiled=True)  13.4 us
    unnamed x31, local copies, waits for them, and re-layouts  11.6 us
  transfers between devices with their start and end apart: 3, of which 2 were waited for; matrix products, arithmetic and copies ran while one was open for 11% of the time, Pallas kernels for 0%

commit v1 on v0

v1 whole, which is shorter than its diff:
```python
import functools
import math

import jax
import jax.numpy as jnp
from jax import lax
from jax.experimental import pallas as pl
from jax.experimental.pallas import tpu as pltpu
from jax.sharding import PartitionSpec as P

BLOCKED = -1e30
MESH = pl.DeviceIdType.MESH


def kernel(
    n,
    dims,
    table,
    lengths,
    sizes,
    q_ref,
    bits_ref,
    keys_hbm,
    values_hbm,
    tree_k,
    tree_v,
    out_ref,
    keys,
    values,
    q_all,
    bits_all,
    part,
    stats,
    got,
    got_stats,
    send,
    send_stats,
    local_sem,
    q_send,
    q_recv,
    bits_send,
    bits_recv,
    o_send,
    o_recv,
    s_send,
    s_recv,
):
    requests, heads, rows, pages, page_len, nodes_dev, words = dims
    me = lax.axis_index("blk")
    last = n - 1
    scale = math.log2(math.e) / math.sqrt(q_ref.shape[-1])

    def dev(at):
        return {"blk": lax.rem(at + n, n)}

    barrier = pltpu.get_barrier_semaphore()
    for step in (1, n - 1):
        pl.semaphore_signal(barrier, inc=1, device_id=dev(me + step), device_id_type=MESH)
    copy_k = pltpu.make_async_copy(keys_hbm, keys, local_sem.at[0])
    copy_v = pltpu.make_async_copy(values_hbm, values, local_sem.at[1])
    copy_k.start()
    copy_v.start()
    pl.semaphore_wait(barrier, 2)

    def q_copy(own, t, r, side, to):
        return pltpu.make_async_remote_copy(
            src_ref=q_ref.at[r] if own else q_all.at[t, r],
            dst_ref=q_all.at[t, r],
            send_sem=q_send.at[side, t, r],
            recv_sem=q_recv.at[t, r],
            device_id=dev(to),
            device_id_type=MESH,
        )

    def bits_copy(own, t, side, to):
        return pltpu.make_async_remote_copy(
            src_ref=bits_ref if own else bits_all.at[t],
            dst_ref=bits_all.at[t],
            send_sem=bits_send.at[side, t],
            recv_sem=bits_recv.at[t],
            device_id=dev(to),
            device_id_type=MESH,
        )

    def o_copy(t, r, side, to):
        return pltpu.make_async_remote_copy(
            src_ref=send.at[t, r],
            dst_ref=got.at[side, t, r],
            send_sem=o_send.at[t, r],
            recv_sem=o_recv.at[side, t, r],
            device_id=dev(to),
            device_id_type=MESH,
        )

    def s_copy(t, r, side, to):
        return pltpu.make_async_remote_copy(
            src_ref=send_stats.at[t, r],
            dst_ref=got_stats.at[side, t, r],
            send_sem=s_send.at[t, r],
            recv_sem=s_recv.at[side, t, r],
            device_id=dev(to),
            device_id_type=MESH,
        )

    def towards(side):
        return me + 1 - 2 * side

    def is_end(side):
        return me == last * (1 - side)

    for side in range(2):

        @pl.when(jnp.logical_not(is_end(side)))
        def _():
            bits_copy(True, me, side, towards(side)).start()
            for r in range(requests):
                q_copy(True, me, r, side, towards(side)).start()

    def attend(t, r, load_q, load_bits):
        node_of = me * nodes_dev + lax.broadcasted_iota(jnp.int32, (nodes_dev, rows), 0)
        picked = jnp.zeros((nodes_dev, rows), jnp.int32)
        for w in range(words):
            moved = jnp.right_shift(
                jnp.broadcast_to(load_bits(r, w), (nodes_dev, rows)), jnp.bitwise_and(node_of, 31)
            )
            picked = picked + jnp.where(
                jnp.right_shift(node_of, 5) == w, jnp.bitwise_and(moved, 1), 0
            )
        allowed = jnp.logical_and(picked > 0, node_of < sizes[r])
        spots = lax.broadcasted_iota(jnp.int32, (page_len, rows), 0)
        left = lengths[r] - me * (pages * page_len)

        def one_head(h, carry):
            q = load_q(r, h)
            contract = (((1,), (1,)), ((), ()))
            tree_s = lax.dot_general(
                tree_k[r, h], q, contract, preferred_element_type=jnp.float32
            )
            tree_s = jnp.where(allowed, tree_s * scale, BLOCKED)
            top = jnp.max(tree_s, axis=0, keepdims=True)
            scores = []
            for j in range(pages):
                s = lax.dot_general(
                    keys[h, table[r, j]], q, contract, preferred_element_type=jnp.float32
                )
                s = jnp.where(spots < left - j * page_len, s * scale, BLOCKED)
                top = jnp.maximum(top, jnp.max(s, axis=0, keepdims=True))
                scores.append(s)
            w = jnp.where(allowed, jnp.exp2(tree_s - top), 0.0)
            total = jnp.sum(w, axis=0, keepdims=True)
            acc = jnp.dot(
                tree_v[r, h], w.astype(jnp.bfloat16), preferred_element_type=jnp.float32
            )
            for j in range(pages):
                w = jnp.where(
                    spots < left - j * page_len, jnp.exp2(scores[j] - top), 0.0
                )
                total = total + jnp.sum(w, axis=0, keepdims=True)
                acc = acc + jnp.dot(
                    values[h, table[r, j]],
                    w.astype(jnp.bfloat16),
                    preferred_element_type=jnp.float32,
                )
            part[t, r, h] = acc
            stats[t, r, 0, pl.ds(h, 1), :] = top
            stats[t, r, 1, pl.ds(h, 1), :] = total
            return carry

        lax.fori_loop(0, heads, one_head, 0)

    def merge(side, t, r):
        def one_head(h, carry):
            mine = stats[t, r, 0, pl.ds(h, 1), :]
            theirs = got_stats[side, t, r, 0, pl.ds(h, 1), :]
            top = jnp.maximum(mine, theirs)
            a = jnp.exp2(mine - top)
            b = jnp.exp2(theirs - top)
            stats[t, r, 0, pl.ds(h, 1), :] = top
            stats[t, r, 1, pl.ds(h, 1), :] = (
                stats[t, r, 1, pl.ds(h, 1), :] * a
                + got_stats[side, t, r, 1, pl.ds(h, 1), :] * b
            )
            part[t, r, h] = part[t, r, h] * a + got[side, t, r, h].astype(jnp.float32) * b
            return carry

        lax.fori_loop(0, heads, one_head, 0)

    def ship(side, t, r):
        send[t, r] = part[t, r].astype(jnp.bfloat16)
        send_stats[t, r] = stats[t, r]
        s_copy(t, r, side, towards(side)).start()
        o_copy(t, r, side, towards(side)).start()

    copy_k.wait()
    copy_v.wait()

    def own_request(r, carry):
        attend(
            me, r, lambda r, h: q_ref[r, h], lambda r, w: bits_ref[r, pl.ds(w, 1), :]
        )
        return carry

    lax.fori_loop(0, requests, own_request, 0)

    def arrivals(d, carry):
        def one_request(r, inner):
            for side in range(2):
                t = me - d + 2 * d * side
                real = jnp.logical_and(t >= 0, t <= last)

                @pl.when(real)
                def _():
                    @pl.when(r == 0)
                    def _():
                        bits_copy(False, t, side, towards(side)).wait_recv()

                    q_copy(False, t, r, side, towards(side)).wait_recv()

                @pl.when(jnp.logical_and(real, jnp.logical_not(is_end(side))))
                def _():
                    @pl.when(r == 0)
                    def _():
                        bits_copy(False, t, side, towards(side)).start()

                    q_copy(False, t, r, side, towards(side)).start()

            def both(side, deep):
                t = me - d + 2 * d * side

                @pl.when(jnp.logical_and(t >= 0, t <= last))
                def _():
                    attend(
                        t,
                        r,
                        lambda r, h: q_all[t, r, h],
                        lambda r, w: bits_all[t, r, pl.ds(w, 1), :],
                    )

                    @pl.when(is_end(side))
                    def _():
                        ship(1 - side, t, r)

                return deep

            lax.fori_loop(0, 2, both, 0)
            return inner

        return lax.fori_loop(0, requests, one_request, carry)

    lax.fori_loop(1, n, arrivals, 0)

    def passing(s, carry):
        def turn(k, deep):
            side = jnp.where(2 * me >= n, 1 - k, k)
            t = jnp.where(side == 0, s, last - s)
            ahead = jnp.where(side == 0, t > me, t < me)
            first = me == last * side

            @pl.when(jnp.logical_and(ahead, jnp.logical_not(first)))
            def _():
                def one_request(r, inner):
                    s_copy(t, r, side, towards(side)).wait_recv()
                    o_copy(t, r, side, towards(side)).wait_recv()
                    merge(side, t, r)
                    ship(side, t, r)
                    return inner

                lax.fori_loop(0, requests, one_request, 0)

            return deep

        return lax.fori_loop(0, 2, turn, carry)

    lax.fori_loop(1, n, passing, 0)

    for r in range(requests):
        for side in range(2):

            @pl.when(me != last * side)
            def _():
                s_copy(me, r, side, towards(side)).wait_recv()
                o_copy(me, r, side, towards(side)).wait_recv()
                merge(side, me, r)

        for h in range(heads):
            scaled = part[me, r, h] / stats[me, r, 1, pl.ds(h, 1), :]
            node_at = me * nodes_dev + lax.broadcasted_iota(
                jnp.int32, scaled.shape, 1
            ) // (rows // nodes_dev)
            scaled = jnp.where(node_at < sizes[r], scaled, 0.0)
            out_ref[r, h] = jnp.transpose(scaled).astype(jnp.bfloat16)

    def finish(t, carry):
        for side in range(2):
            sent = jnp.where(side == 0, t <= me, t >= me)

            @pl.when(jnp.logical_and(sent, jnp.logical_not(is_end(side))))
            def _():
                bits_copy(False, t, side, towards(side)).wait_send()
                for r in range(requests):
                    q_copy(False, t, r, side, towards(side)).wait_send()

        @pl.when(t != me)
        def _():
            for r in range(requests):
                s_copy(t, r, 0, me + 1).wait_send()
                o_copy(t, r, 0, me + 1).wait_send()

        return carry

    lax.fori_loop(0, n, finish, 0)


def shards(
    n,
    queries,
    key_pool,
    value_pool,
    page_table,
    cache_lengths,
    tree_sizes,
    ancestor_bits,
    tree_keys,
    tree_values,
):
    requests, nodes_dev, heads, group_size, head_dim = queries.shape
    words = ancestor_bits.shape[2]
    slots, page_len = key_pool.shape[:2]
    pages = page_table.shape[1]
    rows = nodes_dev * group_size
    q = queries.transpose(0, 2, 1, 3, 4).reshape(requests, heads, rows, head_dim)
    bits = jnp.repeat(ancestor_bits.transpose(0, 2, 1), group_size, axis=2)
    keys = key_pool.transpose(2, 0, 1, 3)
    values = value_pool.transpose(2, 0, 3, 1)
    tree_k = tree_keys.transpose(0, 2, 1, 3)
    tree_v = tree_values.transpose(0, 2, 3, 1)
    dims = (requests, heads, rows, pages, page_len, nodes_dev, words)
    smem = pl.BlockSpec(memory_space=pltpu.SMEM)
    vmem = pl.BlockSpec(memory_space=pltpu.VMEM)
    whole = pl.BlockSpec(memory_space=pl.ANY)
    tile = (head_dim, rows)
    dma = pltpu.SemaphoreType.DMA
    out = pl.pallas_call(
        functools.partial(kernel, n, dims),
        out_shape=jax.ShapeDtypeStruct((requests, heads, rows, head_dim), jnp.bfloat16),
        in_specs=[smem, smem, smem, vmem, vmem, whole, whole, vmem, vmem],
        out_specs=vmem,
        scratch_shapes=[
            pltpu.VMEM(keys.shape, jnp.bfloat16),
            pltpu.VMEM(values.shape, jnp.bfloat16),
            pltpu.VMEM((n, requests, heads, rows, head_dim), jnp.bfloat16),
            pltpu.VMEM((n, requests, words, rows), jnp.int32),
            pltpu.VMEM((n, requests, heads) + tile, jnp.float32),
            pltpu.VMEM((n, requests, 2, heads, rows), jnp.float32),
            pltpu.VMEM((2, n, requests, heads) + tile, jnp.bfloat16),
            pltpu.VMEM((2, n, requests, 2, heads, rows), jnp.float32),
            pltpu.VMEM((n, requests, heads) + tile, jnp.bfloat16),
            pltpu.VMEM((n, requests, 2, heads, rows), jnp.float32),
            dma((2,)),
            dma((2, n, requests)),
            dma((n, requests)),
            dma((2, n)),
            dma((n,)),
            dma((n, requests)),
            dma((2, n, requests)),
            dma((n, requests)),
            dma((2, n, requests)),
        ],
        compiler_params=pltpu.CompilerParams(collective_id=0, has_side_effects=True),
    )(page_table, cache_lengths, tree_sizes, q, bits, keys, values, tree_k, tree_v)
    out = out.reshape(requests, heads, nodes_dev, group_size, head_dim)
    return out.transpose(0, 2, 1, 3, 4)


def solution(mesh):
    placed = (
        P(("groups", "sub"), "blk", "heads", None, None),
        P(("groups", "blk", "sub"), None, "heads", None),
        P(("groups", "blk", "sub"), None, "heads", None),
        P(("groups", "sub"), "blk"),
        P(("groups", "sub")),
        P(("groups", "sub")),
        P(("groups", "sub"), "blk", None),
        P(("groups", "sub"), "blk", "heads", None),
        P(("groups", "sub"), "blk", "heads", None),
    )
    return jax.shard_map(
        functools.partial(shards, mesh.shape["blk"]),
        mesh=mesh,
        in_specs=placed,
        out_specs=P(("groups", "sub"), "blk", "heads", None, None),
        check_vma=False,
    )
```

time: 218 us -> 65.7 us (0.30)
  matrix products: 59.9 us -> 0 us
  Pallas kernels: 0 us -> 52.3 us
  blocking collectives: 49.2 us -> 0 us
  waiting for transfers between devices: 41.9 us -> 0 us
  local copies, waits for them, and re-layouts: 32.4 us -> 13.1 us
  other arithmetic: 18.7 us -> 0 us
  between operations: 13.4 us -> 0.01 us
    dot_general x26 -> x0, matrix products: 59.9 us -> none  [the longest x9 25.2 us: absorb(): jnp.einsum('rhngc,rchd->rhngd', weights.astype(jnp.bfloat16), values, pre...]
    pallas_call x0 -> x1, Pallas kernels: none -> 52.3 us  [shards(): pl.pallas_call(functools.partial(kernel, n, dims), out_shape=jax.ShapeDty...]
    unnamed x5 -> x0, waiting for transfers between devices: 41.6 us -> none
    all_gather x2 -> x0, blocking collectives: 29.2 us -> none  [the longest x1 15.9 us: shards(): lax.all_gather(tree_keys, 'blk', axis=1, tiled=True)]
    pmax x1 -> x0, blocking collectives: 19.9 us -> none  [shards(): row_top = lax.pmax(jnp.maximum(local_top, tree_top), 'blk')]
    convert_element_type x8 -> x0, other arithmetic: 11 us -> none  [absorb(): weights.astype(jnp.bfloat16)]
    gather x2 -> x0, local copies, waits for them, and re-layouts: 8.69 us -> none  [the longest x1 5.15 us: shards(): jnp.take(key_pool, slot_rows, axis=0)]
    dynamic_slice x8 -> x0, local copies, waits for them, and re-layouts: 8.42 us -> none  [attend_one_block(): lax.dynamic_slice_in_dim(values, block_at * block_len, block_len, 1)]
  transfers between devices with their start and end apart: 3 -> 0, of which waited for: 2 -> 0; matrix products, arithmetic and copies ran while one was open for 11% -> 0% of each run, Pallas kernels for 0% -> 0%
where the time goes in v1:
time: 65.7 us; the launch traced here: 65.4 us
  Pallas kernels  52.3 us (80%)
  local copies, waits for them, and re-layouts  13.1 us (20%)
    pallas_call x1, Pallas kernels, shards(): pl.pallas_call(functools.partial(kernel, n, dims), out_shape=jax.ShapeDty...  52.3 us
    unnamed x8, local copies, waits for them, and re-layouts  9.17 us
    transpose x1, local copies, waits for them, and re-layouts, shards(): return out.transpose(0, 2, 1, 3, 4)  1.7 us

profile of v1, /device:TPU:0, one launch (start us, length us, event | category | flops | bytes accessed | tf_op | source)
XLA Modules:
  0.0 65.4 jit_solution(15411965621657444852)
XLA Ops:
  0.0 0.0 copy-start
  0.0 0.8 %broadcast_in_dim.3 = s32[2,2,16,8]{3,2,1,0:T(8,128)S(1)} broadcast(s32[2,2,16]{2,1,0:T(2,128)} %bitcast.25), dimensions={0,1,2} | broadcast | bytes 2304 | tf_op jit(solution)/shard_map/broadcast_in_dim | solution.py:332
  0.8 0.7 %reshape.10.bits_ref = s32[2,2,128]{2,1,0:T(2,128)} reshape(s32[2,2,16,8]{3,2,1,0:T(8,128)S(1)} %broadcast_in_dim.3) | data formatting | bytes 4096 | tf_op jit(solution)/shard_map/reshape | solution.py:332
  1.5 1.4 %copy.27 = bf16[2,16,4,128]{3,1,2,0:T(8,128)(2,1)} copy(bf16[2,16,4,128]{3,2,1,0:T(4,128)(2,1)} %param.16) | data formatting | bytes 65536 | tf_op args[7]
  2.8 0.0 copy-done
  2.8 0.8 %copy_bitcast_fusion.2.q_ref = bf16[2,4,128,128]{3,2,1,0:T(8,128)(2,1)} fusion(bf16[2,16,4,8,128]{4,3,2,1,0:T(8,128)(2,1)S(1)} %copy-done), kind=kLoop, calls=%fused_computation.2 | loop fusion | bytes 524288 | tf_op jit(solution)/shard_map/reshape | solution.py:331
  3.6 1.6 %copy.20 = bf16[2,16,4,128]{1,3,2,0:T(8,128)(2,1)} copy(bf16[2,16,4,128]{3,2,1,0:T(4,128)(2,1)} %param.17) | data formatting | bytes 65536 | tf_op args[8]
  5.2 0.0 copy-start.1
  5.2 3.6 %copy.26 = bf16[16,128,4,128]{3,1,0,2:T(8,128)(2,1)} copy(bf16[16,128,4,128]{3,2,1,0:T(4,128)(2,1)} %param.10) | data formatting | bytes 4194304 | tf_op args[1]
  8.8 0.0 copy-done.1
  8.8 2.6 %copy.18 = bf16[16,128,4,128]{1,3,0,2:T(8,128)(2,1)} copy(bf16[16,128,4,128]{3,2,1,0:T(4,128)(2,1)S(1)} %copy-done.1) | data formatting | bytes 4194304 | tf_op args[2]
  11.4 52.3 %shard_map.91 = bf16[2,4,128,128]{3,2,1,0:T(8,128)(2,1)} custom-call(s32[2,8]{1,0:T(2,128)} %table.1, s32[2]{0:T(128)} %lengths.1, s32[2]{0:T(128)} %sizes.1, bf16[2,4,128,128]{3,2,1,0:T(8,128)(2,1)} %copy_bitcast_fusion.2.q_ref, s32[2,2,128]{2,1,0:T(2,128)} %reshape.10.bits_ref, bf16[4,16,128,128]{3,2,1,0:T(8,128)(2,1)} %bitcast.21, ...), custom_call_target="tpu_custom_call" | custom-call | tf_op jit(solution)/shard_map/pallas_call | solution.py:343
  63.7 1.7 %copy_bitcast_fusion.1 = bf16[2,16,4,8,128]{4,3,2,1,0:T(8,128)(2,1)} fusion(bf16[2,4,128,128]{3,2,1,0:T(8,128)(2,1)} %shard_map.91), kind=kLoop, calls=%fused_computation.1 | loop fusion | bytes 524288 | tf_op jit(solution)/shard_map/transpose | solution.py:372
Async XLA Ops:
  0.0 2.8 %copy-start = (bf16[2,16,4,8,128]{4,3,2,1,0:T(8,128)(2,1)S(1)}, bf16[2,16,4,8,128]{4,3,2,1,0:T(8,128)(2,1)}, u32[]{:S(2)}) copy-start(bf16[2,16,4,8,128]{4,3,2,1,0:T(8,128)(2,1)} %param.9) | copy-start | bytes 786436
  5.2 3.6 %copy-start.1 = (bf16[16,128,4,128]{3,2,1,0:T(4,128)(2,1)S(1)}, bf16[16,128,4,128]{3,2,1,0:T(4,128)(2,1)}, u32[]{:S(2)}) copy-start(bf16[16,128,4,128]{3,2,1,0:T(4,128)(2,1)} %param.11) | copy-start | bytes 6291460

commit v2 on v1

v2 whole, which is shorter than its diff:
```python
import functools
import math

import jax
import jax.numpy as jnp
from jax import lax
from jax.experimental import pallas as pl
from jax.experimental.pallas import tpu as pltpu
from jax.sharding import PartitionSpec as P

BLOCKED = -1e30
MESH = pl.DeviceIdType.MESH


def kernel(
    n,
    dims,
    table,
    lengths,
    sizes,
    q_ref,
    bits_ref,
    keys_hbm,
    values_hbm,
    tree_k_raw,
    tree_v_raw,
    out_ref,
    raw_keys,
    raw_values,
    keys,
    values,
    tree_k,
    tree_v,
    pick,
    q_all,
    bits_all,
    part,
    stats,
    got,
    got_stats,
    send,
    send_stats,
    local_sem,
    q_send,
    q_recv,
    bits_send,
    bits_recv,
    o_send,
    o_recv,
    s_send,
    s_recv,
):
    requests, heads, batch, rows, pages, page_len, nodes_dev, words = dims
    me = lax.axis_index("blk")
    last = n - 1
    width = q_ref.shape[-1]
    chunks = requests * heads // batch
    scale = math.log2(math.e) / math.sqrt(width)
    contract = (((1,), (1,)), ((), ()))

    def dev(at):
        return {"blk": lax.rem(at + n, n)}

    barrier = pltpu.get_barrier_semaphore()
    for step in (1, n - 1):
        pl.semaphore_signal(barrier, inc=1, device_id=dev(me + step), device_id_type=MESH)
    copy_k = pltpu.make_async_copy(keys_hbm, raw_keys, local_sem.at[0])
    copy_v = pltpu.make_async_copy(values_hbm, raw_values, local_sem.at[1])
    copy_k.start()
    copy_v.start()
    pl.semaphore_wait(barrier, 2)

    def q_copy(own, t, c, side, to):
        return pltpu.make_async_remote_copy(
            src_ref=q_ref.at[c] if own else q_all.at[t, c],
            dst_ref=q_all.at[t, c],
            send_sem=q_send.at[side, t, c],
            recv_sem=q_recv.at[t, c],
            device_id=dev(to),
            device_id_type=MESH,
        )

    def bits_copy(own, t, side, to):
        return pltpu.make_async_remote_copy(
            src_ref=bits_ref if own else bits_all.at[t],
            dst_ref=bits_all.at[t],
            send_sem=bits_send.at[side, t],
            recv_sem=bits_recv.at[t],
            device_id=dev(to),
            device_id_type=MESH,
        )

    def o_copy(t, c, side, to):
        return pltpu.make_async_remote_copy(
            src_ref=send.at[t, c],
            dst_ref=got.at[side, t, c],
            send_sem=o_send.at[t, c],
            recv_sem=o_recv.at[side, t, c],
            device_id=dev(to),
            device_id_type=MESH,
        )

    def s_copy(t, c, side, to):
        return pltpu.make_async_remote_copy(
            src_ref=send_stats.at[t, c],
            dst_ref=got_stats.at[side, t, c],
            send_sem=s_send.at[t, c],
            recv_sem=s_recv.at[side, t, c],
            device_id=dev(to),
            device_id_type=MESH,
        )

    def towards(side):
        return me + 1 - 2 * side

    def is_end(side):
        return me == last * (1 - side)

    for side in range(2):

        @pl.when(jnp.logical_not(is_end(side)))
        def _():
            bits_copy(True, me, side, towards(side)).start()
            for c in range(chunks):
                q_copy(True, me, c, side, towards(side)).start()

    def sorter(count):
        row = lax.broadcasted_iota(jnp.int32, (count * heads, count * heads), 0)
        column = lax.broadcasted_iota(jnp.int32, (count * heads, count * heads), 1)
        return (column == (row % count) * heads + row // count).astype(jnp.bfloat16)

    def unit(count):
        row = lax.broadcasted_iota(jnp.int32, (count, count), 0)
        return (row == lax.broadcasted_iota(jnp.int32, (count, count), 1)).astype(jnp.bfloat16)

    def exact(a, b, dims_of=(((1,), (0,)), ((), ()))):
        moved = lax.dot_general(a, b, dims_of, preferred_element_type=jnp.float32)
        return moved.astype(jnp.bfloat16)

    group = pick.shape[0] // heads
    pick[...] = sorter(group)
    tree_sorter = sorter(nodes_dev)
    for r in range(requests):
        by_head = exact(tree_sorter, tree_k_raw[r])
        v_by_head = exact(tree_sorter, tree_v_raw[r])
        for h in range(heads):
            span = slice(h * nodes_dev, (h + 1) * nodes_dev)
            tree_k[r * heads + h] = by_head[span]
            tree_v[r * heads + h] = exact(unit(width), v_by_head[span], contract)
    flip = unit(width)
    copy_k.wait()

    def sort_keys(slot, carry):
        for at in range(page_len // group):
            by_head = exact(
                pick[...], raw_keys[slot, at * group * heads : (at + 1) * group * heads, :]
            )
            for h in range(heads):
                keys[h, slot, at * group : (at + 1) * group, :] = by_head[
                    h * group : (h + 1) * group
                ]
        return carry

    lax.fori_loop(0, raw_keys.shape[0], sort_keys, 0)
    copy_v.wait()

    def sort_values(slot, carry):
        pieces = [
            exact(pick[...], raw_values[slot, at * group * heads : (at + 1) * group * heads, :])
            for at in range(page_len // group)
        ]
        for h in range(heads):
            of_head = jnp.concatenate(
                [piece[h * group : (h + 1) * group] for piece in pieces], axis=0
            )
            values[h, slot] = exact(flip, of_head, contract)
        return carry

    lax.fori_loop(0, raw_values.shape[0], sort_values, 0)

    def attend(t, c, load_q, load_bits):
        r = c * batch // heads
        node_of = me * nodes_dev + lax.broadcasted_iota(
            jnp.int32, (nodes_dev, nodes_dev), 0
        )
        picked = jnp.zeros((nodes_dev, nodes_dev), jnp.int32)
        for w in range(words):
            moved = jnp.right_shift(
                jnp.broadcast_to(load_bits(r, w), (nodes_dev, nodes_dev)),
                jnp.bitwise_and(node_of, 31),
            )
            picked = picked + jnp.where(
                jnp.right_shift(node_of, 5) == w, jnp.bitwise_and(moved, 1), 0
            )
        picked = jnp.where(node_of < sizes[r], picked, 0)
        spread = (
            lax.broadcasted_iota(jnp.int32, (nodes_dev, rows), 0)
            == lax.broadcasted_iota(jnp.int32, (nodes_dev, rows), 1) // (rows // nodes_dev)
        ).astype(jnp.float32)
        allowed = (
            jnp.dot(picked.astype(jnp.float32), spread, preferred_element_type=jnp.float32) > 0.5
        )
        spots = lax.broadcasted_iota(jnp.int32, (page_len, rows), 0)
        left = lengths[r] - me * (pages * page_len)
        firsts = [(c * batch + i) % heads for i in range(batch)]
        tops, all_scores = [], []
        for i in range(batch):
            q = load_q(c, i)
            tree_s = lax.dot_general(
                tree_k[c * batch + i], q, contract, preferred_element_type=jnp.float32
            )
            tree_s = jnp.where(allowed, tree_s * scale, BLOCKED)
            top = jnp.max(tree_s, axis=0, keepdims=True)
            scores = []
            for j in range(pages):
                s = lax.dot_general(
                    keys[firsts[i], table[r, j]], q, contract, preferred_element_type=jnp.float32
                )
                s = jnp.where(spots < left - j * page_len, s * scale, BLOCKED)
                top = jnp.maximum(top, jnp.max(s, axis=0, keepdims=True))
                scores.append(s)
            tops.append(top)
            all_scores.append([tree_s] + scores)
        for i in range(batch):
            top = tops[i]
            w = jnp.exp2(all_scores[i][0] - top)
            total = jnp.sum(w, axis=0, keepdims=True)
            acc = jnp.dot(
                tree_v[c * batch + i], w.astype(jnp.bfloat16), preferred_element_type=jnp.float32
            )
            for j in range(pages):
                w = jnp.exp2(all_scores[i][1 + j] - top)
                total = total + jnp.sum(w, axis=0, keepdims=True)
                acc = acc + jnp.dot(
                    values[firsts[i], table[r, j]],
                    w.astype(jnp.bfloat16),
                    preferred_element_type=jnp.float32,
                )
            part[t, c, i] = acc
            stats[t, c, 0, i : i + 1, :] = top
            stats[t, c, 1, i : i + 1, :] = total

    def merge(side, t, c):
        for i in range(batch):
            mine = stats[t, c, 0, i : i + 1, :]
            theirs = got_stats[side, t, c, 0, i : i + 1, :]
            top = jnp.maximum(mine, theirs)
            a = jnp.exp2(mine - top)
            b = jnp.exp2(theirs - top)
            stats[t, c, 0, i : i + 1, :] = top
            stats[t, c, 1, i : i + 1, :] = (
                stats[t, c, 1, i : i + 1, :] * a + got_stats[side, t, c, 1, i : i + 1, :] * b
            )
            part[t, c, i] = part[t, c, i] * a + got[side, t, c, i].astype(jnp.float32) * b

    def ship(side, t, c):
        send_stats[t, c] = stats[t, c]
        send[t, c] = part[t, c].astype(jnp.bfloat16)
        s_copy(t, c, side, towards(side)).start()
        o_copy(t, c, side, towards(side)).start()

    def arrivals(d, carry):
        def one_chunk(c, inner):
            for side in range(2):
                t = me - d + 2 * d * side
                real = jnp.logical_and(t >= 0, t <= last)

                @pl.when(real)
                def _():
                    @pl.when(c == 0)
                    def _():
                        bits_copy(False, t, side, towards(side)).wait_recv()

                    q_copy(False, t, c, side, towards(side)).wait_recv()

                @pl.when(jnp.logical_and(real, jnp.logical_not(is_end(side))))
                def _():
                    @pl.when(c == 0)
                    def _():
                        bits_copy(False, t, side, towards(side)).start()

                    q_copy(False, t, c, side, towards(side)).start()

            def both(side, deep):
                t = me - d + 2 * d * side

                @pl.when(jnp.logical_and(t >= 0, t <= last))
                def _():
                    attend(
                        t,
                        c,
                        lambda c, i: q_all[t, c, i],
                        lambda r, w: bits_all[t, r, pl.ds(w, 1), :],
                    )

                    @pl.when(is_end(side))
                    def _():
                        ship(1 - side, t, c)

                return deep

            lax.fori_loop(0, 2, both, 0)
            return inner

        return lax.fori_loop(0, chunks, one_chunk, carry)

    lax.fori_loop(1, n, arrivals, 0)

    def own_chunk(c, carry):
        attend(
            me, c, lambda c, i: q_ref[c, i], lambda r, w: bits_ref[r, pl.ds(w, 1), :]
        )
        return carry

    lax.fori_loop(0, chunks, own_chunk, 0)

    def passing(s, carry):
        def turn(k, deep):
            side = jnp.where(2 * me >= n, 1 - k, k)
            t = jnp.where(side == 0, s, last - s)
            ahead = jnp.where(side == 0, t > me, t < me)
            first = me == last * side

            @pl.when(jnp.logical_and(ahead, jnp.logical_not(first)))
            def _():
                def one_chunk(c, inner):
                    s_copy(t, c, side, towards(side)).wait_recv()
                    o_copy(t, c, side, towards(side)).wait_recv()
                    merge(side, t, c)
                    ship(side, t, c)
                    return inner

                lax.fori_loop(0, chunks, one_chunk, 0)

            return deep

        return lax.fori_loop(0, 2, turn, carry)

    lax.fori_loop(1, n, passing, 0)

    def own_result(c, carry):
        for side in range(2):

            @pl.when(me != last * side)
            def _():
                s_copy(me, c, side, towards(side)).wait_recv()
                o_copy(me, c, side, towards(side)).wait_recv()
                merge(side, me, c)

        for i in range(batch):
            scaled = part[me, c, i] / stats[me, c, 1, i : i + 1, :]
            node_at = me * nodes_dev + lax.broadcasted_iota(
                jnp.int32, scaled.shape, 1
            ) // (rows // nodes_dev)
            scaled = jnp.where(node_at < sizes[c * batch // heads], scaled, 0.0)
            out_ref[c, i] = jnp.transpose(scaled).astype(jnp.bfloat16)
        return carry

    lax.fori_loop(0, chunks, own_result, 0)

    def finish(t, carry):
        for side in range(2):
            sent = jnp.where(side == 0, t <= me, t >= me)

            @pl.when(jnp.logical_and(sent, jnp.logical_not(is_end(side))))
            def _():
                bits_copy(False, t, side, towards(side)).wait_send()
                for c in range(chunks):
                    q_copy(False, t, c, side, towards(side)).wait_send()

        @pl.when(t != me)
        def _():
            for c in range(chunks):
                s_copy(t, c, 0, me + 1).wait_send()
                o_copy(t, c, 0, me + 1).wait_send()

        return carry

    lax.fori_loop(0, n, finish, 0)


def shards(
    n,
    queries,
    key_pool,
    value_pool,
    page_table,
    cache_lengths,
    tree_sizes,
    ancestor_bits,
    tree_keys,
    tree_values,
):
    requests, nodes_dev, heads, group_size, head_dim = queries.shape
    words = ancestor_bits.shape[2]
    slots, page_len = key_pool.shape[:2]
    pages = page_table.shape[1]
    rows = nodes_dev * group_size
    batch = max(1, heads // 2)
    chunks = requests * heads // batch
    group = min(page_len, max(1, 256 // heads))
    q = queries.transpose(0, 2, 1, 3, 4).reshape(chunks, batch, rows, head_dim)
    bits = ancestor_bits.transpose(0, 2, 1)
    keys = key_pool.reshape(slots, page_len * heads, head_dim)
    values = value_pool.reshape(slots, page_len * heads, head_dim)
    tree_k = tree_keys.reshape(requests, nodes_dev * heads, head_dim)
    tree_v = tree_values.reshape(requests, nodes_dev * heads, head_dim)
    dims = (requests, heads, batch, rows, pages, page_len, nodes_dev, words)
    smem = pl.BlockSpec(memory_space=pltpu.SMEM)
    vmem = pl.BlockSpec(memory_space=pltpu.VMEM)
    whole = pl.BlockSpec(memory_space=pl.ANY)
    dma = pltpu.SemaphoreType.DMA
    narrow = jnp.bfloat16
    piece = (batch, head_dim, rows)
    note = (2, batch, rows)
    out = pl.pallas_call(
        functools.partial(kernel, n, dims),
        out_shape=jax.ShapeDtypeStruct((chunks, batch, rows, head_dim), narrow),
        in_specs=[smem, smem, smem, vmem, vmem, whole, whole, vmem, vmem],
        out_specs=vmem,
        scratch_shapes=[
            pltpu.VMEM(keys.shape, narrow),
            pltpu.VMEM(values.shape, narrow),
            pltpu.VMEM((heads, slots, page_len, head_dim), narrow),
            pltpu.VMEM((heads, slots, head_dim, page_len), narrow),
            pltpu.VMEM((requests * heads, nodes_dev, head_dim), narrow),
            pltpu.VMEM((requests * heads, head_dim, nodes_dev), narrow),
            pltpu.VMEM((group * heads, group * heads), narrow),
            pltpu.VMEM((n, chunks, batch, rows, head_dim), narrow),
            pltpu.VMEM((n, requests, words, nodes_dev), jnp.int32),
            pltpu.VMEM((n, chunks) + piece, jnp.float32),
            pltpu.VMEM((n, chunks) + note, jnp.float32),
            pltpu.VMEM((2, n, chunks) + piece, narrow),
            pltpu.VMEM((2, n, chunks) + note, jnp.float32),
            pltpu.VMEM((n, chunks) + piece, narrow),
            pltpu.VMEM((n, chunks) + note, jnp.float32),
            dma((2,)),
            dma((2, n, chunks)),
            dma((n, chunks)),
            dma((2, n)),
            dma((n,)),
            dma((n, chunks)),
            dma((2, n, chunks)),
            dma((n, chunks)),
            dma((2, n, chunks)),
        ],
        compiler_params=pltpu.CompilerParams(collective_id=0, has_side_effects=True),
    )(page_table, cache_lengths, tree_sizes, q, bits, keys, values, tree_k, tree_v)
    out = out.reshape(requests, heads, nodes_dev, group_size, head_dim)
    return out.transpose(0, 2, 1, 3, 4)


def solution(mesh):
    placed = (
        P(("groups", "sub"), "blk", "heads", None, None),
        P(("groups", "blk", "sub"), None, "heads", None),
        P(("groups", "blk", "sub"), None, "heads", None),
        P(("groups", "sub"), "blk"),
        P(("groups", "sub")),
        P(("groups", "sub")),
        P(("groups", "sub"), "blk", None),
        P(("groups", "sub"), "blk", "heads", None),
        P(("groups", "sub"), "blk", "heads", None),
    )
    return jax.shard_map(
        functools.partial(shards, mesh.shape["blk"]),
        mesh=mesh,
        in_specs=placed,
        out_specs=P(("groups", "sub"), "blk", "heads", None, None),
        check_vma=False,
    )
```

time: 65.7 us -> 52.6 us (0.80)
  local copies, waits for them, and re-layouts: 13.1 us -> 3.4 us
  Pallas kernels: 52.3 us -> 49 us
    unnamed x8 -> x0, local copies, waits for them, and re-layouts: 9.17 us -> none
    pallas_call x1, Pallas kernels: 52.3 us -> 49 us  [shards(): pl.pallas_call(functools.partial(kernel, n, dims), out_shape=jax.ShapeDty...]
    broadcast_in_dim x1 -> x0, local copies, waits for them, and re-layouts: 0.79 us -> none  [shards(): bits = jnp.repeat(ancestor_bits.transpose(0, 2, 1), group_size, axis=2)]
    reshape x2 -> x1, local copies, waits for them, and re-layouts: 1.41 us -> 1.7 us  [shards(): out = out.reshape(requests, heads, nodes_dev, group_size, head_dim)]
where the time goes in v2:
time: 52.6 us; the launch traced here: 52.4 us
  Pallas kernels  49 us (93%)
  local copies, waits for them, and re-layouts  3.4 us (6%)
    pallas_call x1, Pallas kernels, shards(): pl.pallas_call(functools.partial(kernel, n, dims), out_shape=jax.ShapeDty...  49 us
    transpose x1, local copies, waits for them, and re-layouts, shards(): q = queries.transpose(0, 2, 1, 3, 4).reshape(chunks, batch, rows, head_dim)  1.7 us
    reshape x1, local copies, waits for them, and re-layouts, shards(): out = out.reshape(requests, heads, nodes_dev, group_size, head_dim)  1.7 us

profile of v2, /device:TPU:0, one launch (start us, length us, event | category | flops | bytes accessed | tf_op | source)
XLA Modules:
  0.0 52.4 jit_solution(11304862082341111369)
XLA Ops:
  0.0 1.7 %copy.10 = bf16[2,4,16,8,128]{4,3,2,1,0:T(8,128)(2,1)} copy(bf16[2,4,16,8,128]{4,3,1,2,0:T(8,128)(2,1)} %bitcast.15) | data formatting | bytes 524288 | tf_op jit(solution)/shard_map/transpose | solution.py:402
  1.7 49.0 %shard_map.91 = bf16[4,2,128,128]{3,2,1,0:T(8,128)(2,1)} custom-call(s32[2,8]{1,0:T(2,128)} %table.1, s32[2]{0:T(128)} %lengths.1, s32[2]{0:T(128)} %sizes.1, bf16[4,2,128,128]{3,2,1,0:T(8,128)(2,1)} %bitcast.14, s32[2,2,16]{2,1,0:T(2,128)} %bitcast.18, bf16[16,512,128]{2,1,0:T(8,128)(2,1)} %bitcast.11, bf16[16,512,128]{2,1,0:T(8,128)(2,1)} %bitcast.12, ...), custom_call_target="tpu_custom_call" | custom-call | tf_op jit(solution)/shard_map/pallas_call | solution.py:416
  50.7 1.7 %copy.13 = bf16[2,4,16,8,128]{4,3,1,2,0:T(8,128)(2,1)} copy(bf16[2,4,16,8,128]{4,3,2,1,0:T(8,128)(2,1)} %bitcast.13) | data formatting | bytes 524288 | tf_op jit(solution)/shard_map/reshape | solution.py:449
